TPU v7x, 256 devices: a whole 4x4x8 slice. The times are simulated.
256 devices in a mesh: sa: 32 (over z_lo, x, core), sb: 8 (over z_hi, y).
Axes of the slice: x: 4, y: 4, z: 8 (z_hi: 2, z_lo: 4; z = z_hi * 4 + z_lo), core: 2. Of those that a mesh axis runs over, the one named last changes fastest.
Arguments:
- tokens: bfloat16 [64, 32, 32, 2048], P('sa', 'sb'), may hold values from -6 to 6
- norm_gain: float32 [2048], replicated, may hold values from 0.5 to 1.5
- gate_weight: bfloat16 [2048, 2048], P(('sa', 'sb')), may hold values from -0.125 to 0.125
- level_one: bfloat16 [32, 32, 64, 64], P('sb', 'sa'), may hold values from -0.75 to 0.75
- level_two: bfloat16 [64, 32, 32, 32], P('sa', 'sb'), may hold values from -1 to 1
- level_three: bfloat16 [64, 32, 32, 32], P('sa', 'sb'), may hold values from -1 to 1
- upstream: bfloat16 [64, 32, 32, 2048], P('sa', 'sb'), may hold values from -6 to 6
Outputs:
- output: bfloat16 [64, 32, 32, 2048], P('sa', 'sb')
- grad_tokens: bfloat16 [64, 32, 32, 2048], P('sa', 'sb')
- grad_one: float32 [32, 32, 64, 64], P('sb', 'sa')
- grad_two: float32 [64, 32, 32, 32], P('sa', 'sb')
- grad_three: float32 [64, 32, 32, 32], P('sa', 'sb')
All inputs are finite; a program needn't handle non-finite values.
Results may differ from a plain program's by a relative error of at most 0.0071.
Values may be sent and summed in bfloat16 or wider, within the bound.
A program may use at most 128 MiB of HBM per device.

v0:
```python
import jax
import jax.numpy as jnp
from jax import lax
from jax.sharding import Mesh
from jax.sharding import PartitionSpec as P

SA = ("sa_0", "sa_1", "sa_2")
SB = ("sb_0", "sb_1")
SA_SB = ("sa_0", "sa_1", "sa_2", "sb_0", "sb_1")


EPSILON = 1e-06


def piece_ends(length, count):
    unit = 8 if length >= 8 * count else 1
    return [length // unit * k // count * unit for k in range(1, count)]


def all_blocks(shard, axes, order):
    parts = shard[None]
    for k in order:
        parts = lax.all_gather(parts, axes[k], axis=0, tiled=True)
    block = [lax.axis_size(axes[k]) for k in reversed(order)]
    parts = parts.reshape(*block, *shard.shape)
    turned = sorted(range(len(order)), key=lambda place: order[len(order) - 1 - place])
    return parts.transpose(*turned, *range(len(order), parts.ndim)).reshape(-1, *shard.shape)


def laid_out(parts, dim):
    dims = list(parts.shape[1:])
    dims[dim] *= parts.shape[0]
    return jnp.moveaxis(parts, 0, dim).reshape(dims)


def gather_all_axes(shard, axes, dim):
    widest = max(range(max(1, shard.ndim - 1)), key=lambda d: shard.shape[d])
    count, outs = (len(axes), [])
    for first, share in enumerate(
        jnp.split(shard, piece_ends(shard.shape[widest], count), axis=widest)
    ):
        if share.size:
            order = [(first - k) % count for k in range(count)]
            outs.append(all_blocks(share, axes, order))
    return laid_out(jnp.concatenate(outs, axis=widest + 1), dim)


def across_first(values, handle):
    return handle(lax.all_to_all(values, SA, split_axis=2, concat_axis=0, tiled=True))


def return_first(values):
    return lax.all_to_all(values, SA, split_axis=0, concat_axis=2, tiled=True)


def across_second(values, handle):
    return handle(lax.all_to_all(values, SB, split_axis=2, concat_axis=1, tiled=True))


def return_second(values):
    return lax.all_to_all(values, SB, split_axis=1, concat_axis=2, tiled=True)


def body(tokens, norm_gain, gate_weight, level_one, level_two, level_three, upstream):
    channels = tokens.shape[3]
    tokens_float = tokens.astype(jnp.float32)
    inverse_rms = lax.rsqrt(jnp.mean(tokens_float * tokens_float, axis=3, keepdims=True) + EPSILON)
    normed = (tokens_float * inverse_rms * norm_gain).astype(jnp.bfloat16)
    token_rows = normed.reshape(-1, channels)
    gathered = gather_all_axes(gate_weight, SA_SB, 0)
    gate_pre = jnp.dot(token_rows, gathered, preferred_element_type=jnp.float32)
    gate_pre = gate_pre.reshape(tokens.shape)

    def first_level(spread):
        blended = jnp.einsum(
            "jkoi,ijkc->ojkc", level_one, spread, preferred_element_type=jnp.float32
        )
        return (return_first(blended.astype(jnp.bfloat16)), spread)

    first_mix, spread_one = across_first(normed, first_level)

    def second_level(spread):
        blended = jnp.einsum(
            "ikoj,ijkc->iokc", level_two, spread, preferred_element_type=jnp.float32
        )
        return (return_second(blended.astype(jnp.bfloat16)), spread)

    second_mix, spread_two = across_second(first_mix, second_level)
    mixed_all = jnp.einsum(
        "ijok,ijkc->ijoc", level_three, second_mix, preferred_element_type=jnp.float32
    )
    gate_sigmoid = jax.nn.sigmoid(gate_pre)
    gate_value = gate_pre * gate_sigmoid
    output = (tokens_float + mixed_all * gate_value).astype(jnp.bfloat16)
    upstream_float = upstream.astype(jnp.float32)
    grad_mixed = (upstream_float * gate_value).astype(jnp.bfloat16)
    grad_gate = (
        upstream_float * mixed_all * gate_sigmoid * (1.0 + gate_pre * (1.0 - gate_sigmoid))
    ).astype(jnp.bfloat16)
    grad_scale = channels ** (-0.5)
    grad_three = (
        jnp.einsum("ijoc,ijkc->ijok", grad_mixed, second_mix, preferred_element_type=jnp.float32)
        * grad_scale
    )
    grad_second = jnp.einsum(
        "ijok,ijoc->ijkc", level_three, grad_mixed, preferred_element_type=jnp.float32
    ).astype(jnp.bfloat16)

    def second_back(spread):
        blended = jnp.einsum(
            "ikoj,iokc->ijkc", level_two, spread, preferred_element_type=jnp.float32
        )
        return (return_second(blended.astype(jnp.bfloat16)), spread)

    grad_first, grad_spread_two = across_second(grad_second, second_back)
    grad_two = (
        jnp.einsum(
            "iokc,ijkc->ikoj", grad_spread_two, spread_two, preferred_element_type=jnp.float32
        )
        * grad_scale
    )

    def first_back(spread):
        blended = jnp.einsum(
            "jkoi,ojkc->ijkc", level_one, spread, preferred_element_type=jnp.float32
        )
        return (return_first(blended.astype(jnp.bfloat16)), spread)

    grad_normed, grad_spread_one = across_first(grad_first, first_back)
    grad_one = (
        jnp.einsum(
            "ojkc,ijkc->jkoi", grad_spread_one, spread_one, preferred_element_type=jnp.float32
        )
        * grad_scale
    )
    grad_rows = grad_gate.reshape(-1, channels)
    back_term = jnp.einsum("tc,rc->tr", grad_rows, gathered, preferred_element_type=jnp.float32)
    grad_hidden = grad_normed.astype(jnp.float32) + back_term.reshape(tokens.shape)
    weighted = grad_hidden * norm_gain
    average = jnp.mean(weighted * tokens_float, axis=3, keepdims=True)
    grad_tokens = (
        upstream_float + inverse_rms * weighted - tokens_float * inverse_rms**3 * average
    ).astype(jnp.bfloat16)
    return (output, grad_tokens, grad_one, grad_two, grad_three)


def solution(mesh):
    split = Mesh(mesh.devices.reshape(4, 4, 2, 2, 4), ("sa_0", "sa_1", "sa_2", "sb_0", "sb_1"))
    in_specs = (
        P(SA, SB, None, None),
        P(),
        P(SA_SB, None),
        P(SB, SA, None, None),
        P(SA, SB, None, None),
        P(SA, SB, None, None),
        P(SA, SB, None, None),
    )
    out_specs = (
        P(SA, SB, None, None),
        P(SA, SB, None, None),
        P(SB, SA, None, None),
        P(SA, SB, None, None),
        P(SA, SB, None, None),
    )
    return jax.shard_map(body, mesh=split, in_specs=in_specs, out_specs=out_specs, check_vma=False)
```

profile of v0, /device:TPU:9, one launch (start us, length us, event | category | flops | bytes accessed | tf_op | source)
XLA Modules:
  0.0 572.6 jit_solution(2166422184694849511)
XLA Ops:
  8.1 9.4 %all-gather.15 = bf16[4,2,2048]{2,1,0:T(2,128)(2,1)S(1)} all-gather(bf16[1,2,2048]{2,1,0:T(2,128)(2,1)S(1)} %get-tuple-element.23), channel_id=7, replica_groups=mesh['sa_0'=4,'sa_1'=4,'sa_2'=2,'sb_0'=2,'sb_1'=4] {'sa_1'}, dimensions={0}, use_global_device_ids=true | all-gather | bytes 40960 | tf_op jit(solution)/shard_map/all_gather | solution.py:23
  17.5 11.5 %all_gather.81 = bf16[16,2,2048]{2,1,0:T(2,128)(2,1)S(1)} all-gather(bf16[4,2,2048]{2,1,0:T(2,128)(2,1)S(1)} %all-gather.15), channel_id=1, replica_groups=mesh['sa_0'=4,'sa_1'=4,'sa_2'=2,'sb_0'=2,'sb_1'=4] {'sa_0'}, dimensions={0}, use_global_device_ids=true | all-gather | bytes 163840 | tf_op jit(solution)/shard_map/all_gather | solution.py:23
  29.1 11.1 %all_gather.82 = bf16[64,2,2048]{2,1,0:T(2,128)(2,1)} all-gather(bf16[16,2,2048]{2,1,0:T(2,128)(2,1)S(1)} %all_gather.81), channel_id=1, replica_groups=mesh['sa_0'=4,'sa_1'=4,'sa_2'=2,'sb_0'=2,'sb_1'=4] {'sb_1'}, dimensions={0}, use_global_device_ids=true | all-gather | bytes 655360 | tf_op jit(solution)/shard_map/all_gather | solution.py:23
  41.1 10.4 %all-gather.16 = bf16[2,1,2048]{2,1,0:T(2,128)(2,1)S(1)} all-gather(bf16[1,1,2048]{2,1,0:T(2,128)(2,1)S(1)} %get-tuple-element.25), channel_id=8, replica_groups=mesh['sa_0'=4,'sa_1'=4,'sa_2'=2,'sb_0'=2,'sb_1'=4] {'sa_2'}, dimensions={0}, use_global_device_ids=true | all-gather | bytes 12288 | tf_op jit(solution)/shard_map/all_gather | solution.py:23
  51.5 9.0 %all-gather.17 = bf16[4,2,2048]{2,1,0:T(2,128)(2,1)S(1)} all-gather(bf16[1,2,2048]{2,1,0:T(2,128)(2,1)S(1)} %bitcast.145), channel_id=9, replica_groups=mesh['sa_0'=4,'sa_1'=4,'sa_2'=2,'sb_0'=2,'sb_1'=4] {'sa_1'}, dimensions={0}, use_global_device_ids=true | all-gather | bytes 40960 | tf_op jit(solution)/shard_map/all_gather | solution.py:23
  60.6 14.8 %all-gather.8 = bf16[32,2048]{1,0:T(8,128)(2,1)S(1)} all-gather(bf16[8,2048]{1,0:T(8,128)(2,1)S(1)} %reshape.128), channel_id=10, replica_groups=mesh['sa_0'=4,'sa_1'=4,'sa_2'=2,'sb_0'=2,'sb_1'=4] {'sa_0'}, dimensions={0}, use_global_device_ids=true | all-gather | bytes 163840 | tf_op jit(solution)/shard_map/all_gather | solution.py:23
  75.4 12.1 %all-gather.9 = bf16[128,2048]{1,0:T(8,128)(2,1)} all-gather(bf16[32,2048]{1,0:T(8,128)(2,1)S(1)} %all-gather.8), channel_id=11, replica_groups=mesh['sa_0'=4,'sa_1'=4,'sa_2'=2,'sb_0'=2,'sb_1'=4] {'sb_1'}, dimensions={0}, use_global_device_ids=true | all-gather | bytes 655360 | tf_op jit(solution)/shard_map/all_gather | solution.py:23
  87.6 11.5 %all-gather.13 = bf16[4,1,2048]{2,1,0:T(2,128)(2,1)S(1)} all-gather(bf16[1,1,2048]{2,1,0:T(2,128)(2,1)S(1)} %get-tuple-element.26), channel_id=2, replica_groups=mesh['sa_0'=4,'sa_1'=4,'sa_2'=2,'sb_0'=2,'sb_1'=4] {'sa_0'}, dimensions={0}, use_global_device_ids=true | all-gather | bytes 20480 | tf_op jit(solution)/shard_map/all_gather | solution.py:23
  99.1 9.0 %all-gather.14 = bf16[4,4,2048]{2,1,0:T(4,128)(2,1)S(1)} all-gather(bf16[1,4,2048]{2,1,0:T(4,128)(2,1)S(1)} %bitcast.144), channel_id=3, replica_groups=mesh['sa_0'=4,'sa_1'=4,'sa_2'=2,'sb_0'=2,'sb_1'=4] {'sb_1'}, dimensions={0}, use_global_device_ids=true | all-gather | bytes 81920 | tf_op jit(solution)/shard_map/all_gather | solution.py:23
  115.9 32.1 %all-gather.3 = bf16[64,2048]{1,0:T(8,128)(2,1)} all-gather(bf16[32,2048]{1,0:T(8,128)(2,1)S(1)} %all-gather.2), channel_id=5, replica_groups=mesh['sa_0'=4,'sa_1'=4,'sa_2'=2,'sb_0'=2,'sb_1'=4] {'sa_2'}, dimensions={0}, use_global_device_ids=true | all-gather | bytes 393216 | tf_op jit(solution)/shard_map/all_gather | solution.py:23
  155.3 18.4 %all-gather.18 = bf16[2,2,2048]{2,1,0:T(2,128)(2,1)S(1)} all-gather(bf16[1,2,2048]{2,1,0:T(2,128)(2,1)S(1)} %get-tuple-element.24), channel_id=13, replica_groups=mesh['sa_0'=4,'sa_1'=4,'sa_2'=2,'sb_0'=2,'sb_1'=4] {'sb_0'}, dimensions={0}, use_global_device_ids=true | all-gather | bytes 24576 | tf_op jit(solution)/shard_map/all_gather | solution.py:23
  175.9 10.1 %all_gather.92 = bf16[16,2,2048]{2,1,0:T(2,128)(2,1)S(1)} all-gather(bf16[4,2,2048]{2,1,0:T(2,128)(2,1)S(1)} %all_gather.91), channel_id=1, replica_groups=mesh['sa_0'=4,'sa_1'=4,'sa_2'=2,'sb_0'=2,'sb_1'=4] {'sa_1'}, dimensions={0}, use_global_device_ids=true | all-gather | bytes 163840 | tf_op jit(solution)/shard_map/all_gather | solution.py:23
  186.0 12.7 %all_gather.93 = bf16[64,2,2048]{2,1,0:T(2,128)(2,1)} all-gather(bf16[16,2,2048]{2,1,0:T(2,128)(2,1)S(1)} %all_gather.92), channel_id=1, replica_groups=mesh['sa_0'=4,'sa_1'=4,'sa_2'=2,'sb_0'=2,'sb_1'=4] {'sa_0'}, dimensions={0}, use_global_device_ids=true | all-gather | bytes 655360 | tf_op jit(solution)/shard_map/all_gather | solution.py:23
  201.1 38.6 %all_to_all.129 = bf16[64,4,1,2048]{3,1,2,0:T(4,128)(2,1)S(1)} all-to-all(bf16[64,4,1,2048]{3,1,2,0:T(4,128)(2,1)S(1)} %copy.42), channel_id=1, replica_groups=mesh['sa_0'=4,'sa_1'=4,'sa_2'=2,'sb_0'=2,'sb_1'=4] {'sa_0','sa_1','sa_2'}, dimensions={0} | all-to-all | bytes 2097152 | tf_op jit(solution)/shard_map/all_to_all | solution.py:53
  250.4 15.1 %all-gather.19 = bf16[4,2,2048]{2,1,0:T(2,128)(2,1)S(1)} all-gather(bf16[1,2,2048]{2,1,0:T(2,128)(2,1)S(1)} %get-tuple-element.22), channel_id=14, replica_groups=mesh['sa_0'=4,'sa_1'=4,'sa_2'=2,'sb_0'=2,'sb_1'=4] {'sb_1'}, dimensions={0}, use_global_device_ids=true | all-gather | bytes 40960 | tf_op jit(solution)/shard_map/all_gather | solution.py:23
  265.5 14.4 %all_gather.96 = bf16[8,2,2048]{2,1,0:T(2,128)(2,1)S(1)} all-gather(bf16[4,2,2048]{2,1,0:T(2,128)(2,1)S(1)} %all-gather.19), channel_id=1, replica_groups=mesh['sa_0'=4,'sa_1'=4,'sa_2'=2,'sb_0'=2,'sb_1'=4] {'sb_0'}, dimensions={0}, use_global_device_ids=true | all-gather | bytes 98304 | tf_op jit(solution)/shard_map/all_gather | solution.py:23
  281.9 10.6 %all_gather.98 = bf16[64,2,2048]{2,1,0:T(2,128)(2,1)} all-gather(bf16[16,2,2048]{2,1,0:T(2,128)(2,1)S(1)} %all_gather.97), channel_id=1, replica_groups=mesh['sa_0'=4,'sa_1'=4,'sa_2'=2,'sb_0'=2,'sb_1'=4] {'sa_1'}, dimensions={0}, use_global_device_ids=true | all-gather | bytes 655360 | tf_op jit(solution)/shard_map/all_gather | solution.py:23
  295.6 9.1 %all-to-all-start.3 = ((bf16[2,32,4,2048]{3,2,0,1:T(4,128)(2,1)}), bf16[2,32,4,2048]{3,2,0,1:T(4,128)(2,1)}, u32[]{:S(2)}, u32[]{:S(2)}) async-start(bf16[2,32,4,2048]{3,2,0,1:T(4,128)(2,1)} %copy.45), calls=%async_computation.3 | async-start | bytes 2097152 | tf_op jit(solution)/shard_map/all_to_all | solution.py:61
  332.0 31.7 %all-gather.33.cloned.1.call-done = bf16[256,2,2048]{2,1,0:T(2,128)(2,1)} async-done(((bf16[64,2,2048]{2,1,0:T(2,128)(2,1)}), bf16[256,2,2048]{2,1,0:T(2,128)(2,1)}) %all-gather.33.cloned.1.call-update) | async-done | bytes 2097168 | tf_op jit(solution)/shard_map/all_gather | solution.py:23
  363.7 37.8 %concatenate.3 = bf16[256,8,2048]{2,1,0:T(8,128)(2,1)} concatenate(bf16[256,1,2048]{2,1,0:T(2,128)(2,1)} %reshape.139, bf16[256,2,2048]{2,1,0:T(2,128)(2,1)} %bitcast.126, bf16[256,1,2048]{2,1,0:T(2,128)(2,1)} %reshape.140, bf16[256,2,2048]{2,1,0:T(2,128)(2,1)} %bitcast.127, bf16[256,2,2048]{2,1,0:T(2,128)(2,1)} %all-gather.33.cloned.1.call-done), dimensions={1} | concatenate | bytes 16777216 | tf_op jit(solution)/shard_map/concatenate | solution.py:45
  416.9 25.3 %all_to_all.130 = bf16[2,4,32,2048]{3,1,0,2:T(4,128)(2,1)S(1)} all-to-all(bf16[2,4,32,2048]{3,1,0,2:T(4,128)(2,1)S(1)} %copy.54), channel_id=1, replica_groups=mesh['sa_0'=4,'sa_1'=4,'sa_2'=2,'sb_0'=2,'sb_1'=4] {'sb_0','sb_1'}, dimensions={2} | all-to-all | bytes 2097152 | tf_op jit(solution)/shard_map/all_to_all | solution.py:57
  446.3 16.8 %all_to_all.131 = bf16[2,32,4,2048]{3,2,0,1:T(4,128)(2,1)S(1)} all-to-all(bf16[2,32,4,2048]{3,2,0,1:T(4,128)(2,1)S(1)} %copy.57), channel_id=1, replica_groups=mesh['sa_0'=4,'sa_1'=4,'sa_2'=2,'sb_0'=2,'sb_1'=4] {'sb_0','sb_1'}, dimensions={1} | all-to-all | bytes 2097152 | tf_op jit(solution)/shard_map/all_to_all | solution.py:61
  464.7 53.5 %all_to_all.132 = bf16[2,4,32,2048]{3,1,0,2:T(4,128)(2,1)S(1)} all-to-all(bf16[2,4,32,2048]{3,1,0,2:T(4,128)(2,1)S(1)} %copy.59), channel_id=1, replica_groups=mesh['sa_0'=4,'sa_1'=4,'sa_2'=2,'sb_0'=2,'sb_1'=4] {'sa_0','sa_1','sa_2'}, dimensions={2} | all-to-all | bytes 2097152 | tf_op jit(solution)/shard_map/all_to_all | solution.py:49
  533.0 21.3 %all-to-all-done.7 = bf16[64,4,1,2048]{3,1,2,0:T(4,128)(2,1)} async-done(((bf16[64,4,1,2048]{3,1,2,0:T(4,128)(2,1)}), bf16[64,4,1,2048]{3,1,2,0:T(4,128)(2,1)}, u32[]{:S(2)}, u32[]{:S(2)}) %all-to-all-start.7) | async-done | bytes 1048608 | tf_op jit(solution)/shard_map/all_to_all | solution.py:53
  (102 shorter events, 111.7 us)
Async XLA Ops:
  7.2 398.5 %copy-start = (bf16[2,4,32,32]{3,2,1,0:T(8,128)(2,1)S(1)}, bf16[2,4,32,32]{3,2,1,0:T(8,128)(2,1)}, u32[]{:S(2)}) copy-start(bf16[2,4,32,32]{3,2,1,0:T(8,128)(2,1)} %param.12) | copy-start | bytes 49156
  7.2 140.9 %copy-start.1 = (bf16[2,4,32,2048]{3,2,1,0:T(8,128)(2,1)S(1)}, bf16[2,4,32,2048]{3,2,1,0:T(8,128)(2,1)}, u32[]{:S(2)}) copy-start(bf16[2,4,32,2048]{3,2,1,0:T(8,128)(2,1)} %param.7) | copy-start | bytes 3145732
  7.2 141.2 %all-gather.27.cloned.1.call-start = ((), (), s32[]{:S(2)}) async-start(), calls=%async_computation.8 | async-start | bytes 1572864 | tf_op jit(solution)/shard_map/all_gather | solution.py:23
  40.2 264.5 %all-gather.37.cloned.1.call-start = ((), (), s32[]{:S(2)}) async-start(), calls=%async_computation.13 | async-start | bytes 1572864 | tf_op jit(solution)/shard_map/all_gather | solution.py:23
  75.4 73.2 %copy-start.14 = (f32[2048]{0:T(1024)S(1)}, f32[2048]{0:T(1024)}, u32[]{:S(2)}) copy-start(f32[2048]{0:T(1024)} %param.8) | copy-start | bytes 24580
  87.5 225.6 %all-gather.35.cloned.1.call-start = ((), (), s32[]{:S(2)}) async-start(), calls=%async_computation.12 | async-start | bytes 1310720 | tf_op jit(solution)/shard_map/all_gather | solution.py:23
  148.0 173.1 %all-gather.29.cloned.1.call-start = ((), (), s32[]{:S(2)}) async-start(), calls=%async_computation.9 | async-start | bytes 3145728 | tf_op jit(solution)/shard_map/all_gather | solution.py:23
  150.7 48.1 %copy-start.13 = (bf16[4,1,64,64]{3,2,1,0:T(8,128)(2,1)S(1)}, bf16[4,1,64,64]{3,2,1,0:T(8,128)(2,1)}, u32[]{:S(2)}) copy-start(bf16[4,1,64,64]{3,2,1,0:T(8,128)(2,1)} %param.10) | copy-start | bytes 98308
  150.7 48.0 %all-to-all-start = ((bf16[2,4,32,2048]{3,1,0,2:T(4,128)(2,1)}), bf16[2,4,32,2048]{3,1,0,2:T(4,128)(2,1)S(1)}, u32[]{:S(2)}, u32[]{:S(2)}) async-start(bf16[2,4,32,2048]{3,1,0,2:T(4,128)(2,1)} %copy.40), calls=%async_computation | async-start | bytes 2097152 | tf_op jit(solution)/shard_map/all_to_all | solution.py:49
  155.2 171.3 %all-gather.31.cloned.1.call-start = ((), (), s32[]{:S(2)}) async-start(), calls=%async_computation.10 | async-start | bytes 2621440 | tf_op jit(solution)/shard_map/all_gather | solution.py:23
  198.8 2.3 copy-start.3
  241.8 50.7 %all-to-all-start.2 = ((bf16[2,4,32,2048]{3,0,1,2:T(2,128)(2,1)}), bf16[2,4,32,2048]{3,0,1,2:T(2,128)(2,1)S(1)}, u32[]{:S(2)}, u32[]{:S(2)}) async-start(bf16[2,4,32,2048]{3,0,1,2:T(2,128)(2,1)} %bitcast.123), calls=%async_computation.2 | async-start | bytes 2097152 | tf_op jit(solution)/shard_map/all_to_all | solution.py:57
  250.4 113.3 %all-gather.33.cloned.1.call-start = ((), (), s32[]{:S(2)}) async-start(), calls=%async_computation.11 | async-start | bytes 2621440 | tf_op jit(solution)/shard_map/all_gather | solution.py:23
  295.6 106.0 %all-to-all-start.3 = ((bf16[2,32,4,2048]{3,2,0,1:T(4,128)(2,1)}), bf16[2,32,4,2048]{3,2,0,1:T(4,128)(2,1)}, u32[]{:S(2)}, u32[]{:S(2)}) async-start(bf16[2,32,4,2048]{3,2,0,1:T(4,128)(2,1)} %copy.45), calls=%async_computation.3 | async-start | bytes 2097152 | tf_op jit(solution)/shard_map/all_to_all | solution.py:61
  405.7 1.2 copy-start.10
  406.9 8.7 %copy-start.8 = (f32[2,4,32,2048]{3,2,1,0:T(8,128)}, f32[2,4,32,2048]{3,2,1,0:T(8,128)S(1)}, u32[]{:S(2)}) copy-start(f32[2,4,32,2048]{3,2,1,0:T(8,128)S(1)} %convolution_bitcast_fusion) | copy-start | bytes 6291460
  415.6 1.3 copy-start.5
  518.2 1.0 copy-start.6
  522.4 31.9 %all-to-all-start.7 = ((bf16[64,4,1,2048]{3,1,2,0:T(4,128)(2,1)}), bf16[64,4,1,2048]{3,1,2,0:T(4,128)(2,1)}, u32[]{:S(2)}, u32[]{:S(2)}) async-start(bf16[64,4,1,2048]{3,1,2,0:T(4,128)(2,1)} %copy.62), calls=%async_computation.7 | async-start | bytes 2097152 | tf_op jit(solution)/shard_map/all_to_all | solution.py:53
  527.6 3.5 copy-start.4
  527.6 3.5 copy-start.7
  533.0 22.7 %copy-start.2 = (bf16[2,4,32,2048]{3,2,1,0:T(8,128)(2,1)S(1)}, bf16[2,4,32,2048]{3,2,1,0:T(8,128)(2,1)}, u32[]{:S(2)}) copy-start(bf16[2,4,32,2048]{3,2,1,0:T(8,128)(2,1)} %param.7) | copy-start | bytes 3145732
  533.0 22.8 %copy-start.9 = (f32[2,4,32,2048]{3,2,1,0:T(8,128)S(1)}, f32[2,4,32,2048]{3,2,1,0:T(8,128)}, u32[]{:S(2)}) copy-start(f32[2,4,32,2048]{3,2,1,0:T(8,128)} %copy-done.8) | copy-start | bytes 6291460
  555.8 8.4 %copy-start.11 = (bf16[2,4,32,2048]{3,2,1,0:T(8,128)(2,1)S(1)}, bf16[2,4,32,2048]{3,2,1,0:T(8,128)(2,1)}, u32[]{:S(2)}) copy-start(bf16[2,4,32,2048]{3,2,1,0:T(8,128)(2,1)} %param.13) | copy-start | bytes 3145732
  (1 other events, 0.9 us)
Sparse Core Ops, SparseCore 0:
  40.4 52.9 all-gather.26
  95.2 50.7 all-gather.36
  148.1 28.8 all-gather.34
  178.6 14.8 all-gather.28
  198.9 37.6 all-gather.30
  292.6 71.0 all-gather.32
where the time goes:
time: 581 us; the launch traced here: 573 us
  blocking collectives  359 us (62%)
  local copies, waits for them, and re-layouts  87.8 us (15%)
  waiting for transfers between devices  53.3 us (9%)
  starting transfers between devices  27.6 us (5%)
  matrix products  27.1 us (5%)
  between operations  14.4 us (2%)
    all_gather x19, blocking collectives, all_blocks(): parts = lax.all_gather(parts, axes[k], axis=0, tiled=True)  224 us
    all_to_all x1, blocking collectives, across_first(): lax.all_to_all(values, SA, split_axis=2, concat_axis=0, tiled=True)  53.5 us
    all_to_all x1, blocking collectives, return_first(): return lax.all_to_all(values, SA, split_axis=0, concat_axis=2, tiled=True)  38.6 us
    concatenate x1, local copies, waits for them, and re-layouts, gather_all_axes(): return laid_out(jnp.concatenate(outs, axis=widest + 1), dim)  37.8 us
    all_gather x6, waiting for transfers between devices, all_blocks(): parts = lax.all_gather(parts, axes[k], axis=0, tiled=True)  31.8 us
    all_to_all x1, blocking collectives, across_second(): lax.all_to_all(values, SB, split_axis=2, concat_axis=1, tiled=True)  25.3 us
    all_to_all x1, waiting for transfers between devices, return_first(): return lax.all_to_all(values, SA, split_axis=0, concat_axis=2, tiled=True)  21.3 us
    all_to_all x1, blocking collectives, return_second(): return lax.all_to_all(values, SB, split_axis=1, concat_axis=2, tiled=True)  16.8 us
  transfers between devices with their start and end apart: 10, of which 2 were waited for; matrix products, arithmetic and copies ran while one was open for 14% of the time, Pallas kernels for 0%

commit v1 on v0

v1 whole, which is shorter than its diff:
```python
import jax
import jax.numpy as jnp
from jax import lax
from jax.sharding import PartitionSpec as P

ALL = ("sa", "sb")
EPSILON = 1e-06


def to_blocks(values):
    i, j, k, c = values.shape
    sa, sb = lax.axis_size("sa"), lax.axis_size("sb")
    parts = values.reshape(i, j, sa, sb, c // sb).transpose(2, 3, 0, 1, 4)
    parts = parts.reshape(sa * sb, i * j, c // sb)
    parts = lax.all_to_all(parts, ALL, split_axis=0, concat_axis=0, tiled=True)
    parts = parts.reshape(sa, sb, i, j, c // sb).transpose(0, 2, 1, 3, 4)
    return parts.reshape(sa * i, sb * j, c // sb)


def from_blocks(values):
    sa, sb = lax.axis_size("sa"), lax.axis_size("sb")
    i, j, c = values.shape[0] // sa, values.shape[1] // sb, values.shape[2]
    parts = values.reshape(sa, i, sb, j, c).transpose(0, 2, 1, 3, 4)
    parts = parts.reshape(sa * sb, i * j, c)
    parts = lax.all_to_all(parts, ALL, split_axis=0, concat_axis=0, tiled=True)
    parts = parts.reshape(sa, sb, i, j, c).transpose(2, 3, 0, 1, 4)
    return parts.reshape(i, j, sa, sb * c)


def dot(pattern, left, right):
    return jnp.einsum(pattern, left, right, preferred_element_type=jnp.float32)


def body(tokens, norm_gain, gate_weight, level_one, level_two, level_three, upstream):
    channels = tokens.shape[3]
    sa, sb = lax.axis_size("sa"), lax.axis_size("sb")
    grad_scale = channels ** (-0.5)
    gathered = lax.all_gather(gate_weight, ALL, axis=0, tiled=True)

    block_one = lax.all_gather(level_one[:, 0], "sb", axis=0, tiled=True)
    block_two = lax.all_gather(level_two, "sb", axis=1, tiled=True)
    block_two = lax.all_to_all(block_two, "sa", split_axis=1, concat_axis=0, tiled=True)[:, 0]

    tokens_float = tokens.astype(jnp.float32)
    inverse_rms = lax.rsqrt(jnp.mean(tokens_float * tokens_float, axis=3, keepdims=True) + EPSILON)
    normed = (tokens_float * inverse_rms * norm_gain).astype(jnp.bfloat16)

    normed_block = to_blocks(normed)
    first_mix = dot("joi,ijc->ojc", block_one, normed_block).astype(jnp.bfloat16)
    second_mix = dot("ioj,ijc->ioc", block_two, first_mix).astype(jnp.bfloat16)
    second_mix = from_blocks(second_mix)
    mixed_all = dot("ijok,ijkc->ijoc", level_three, second_mix)

    token_rows = normed.reshape(-1, channels)
    gate_pre = dot("tr,rc->tc", token_rows, gathered).reshape(tokens.shape)
    gate_sigmoid = jax.nn.sigmoid(gate_pre)
    gate_value = gate_pre * gate_sigmoid
    output = (tokens_float + mixed_all * gate_value).astype(jnp.bfloat16)
    upstream_float = upstream.astype(jnp.float32)
    grad_mixed = (upstream_float * gate_value).astype(jnp.bfloat16)
    grad_gate = (
        upstream_float * mixed_all * gate_sigmoid * (1.0 + gate_pre * (1.0 - gate_sigmoid))
    ).astype(jnp.bfloat16)
    grad_second = dot("ijok,ijoc->ijkc", level_three, grad_mixed).astype(jnp.bfloat16)

    grad_block = to_blocks(grad_second)
    grad_first = dot("ioj,ioc->ijc", block_two, grad_block).astype(jnp.bfloat16)
    grad_normed = dot("joi,ojc->ijc", block_one, grad_first).astype(jnp.bfloat16)
    grad_normed = from_blocks(grad_normed)

    grad_three = dot("ijoc,ijkc->ijok", grad_mixed, second_mix) * grad_scale
    part_two = dot("ioc,ijc->ioj", grad_block, first_mix).astype(jnp.bfloat16)
    part_one = dot("ojc,ijc->joi", grad_first, normed_block).astype(jnp.bfloat16)
    part_two = lax.all_to_all(part_two[:, None], "sa", split_axis=0, concat_axis=1, tiled=True)
    m1, m2 = part_one.shape[1], part_two.shape[2]
    own_i, own_k = part_two.shape[0], part_two.shape[1] // sb
    own_j = part_one.shape[0] // sb
    packed = jnp.concatenate(
        [
            part_one.reshape(sb, -1),
            part_two.reshape(own_i, sb, own_k, m2, m2).transpose(1, 0, 2, 3, 4).reshape(sb, -1),
        ],
        axis=1,
    )
    packed = lax.all_to_all(packed, "sb", split_axis=0, concat_axis=0, tiled=True)
    summed = jnp.sum(packed.astype(jnp.float32), axis=0) * grad_scale
    cut = own_j * m1 * m1
    grad_one = summed[:cut].reshape(own_j, 1, m1, m1)
    grad_two = summed[cut:].reshape(own_i, own_k, m2, m2)

    back_term = dot("tc,rc->tr", grad_gate.reshape(-1, channels), gathered)
    grad_hidden = grad_normed.astype(jnp.float32) + back_term.reshape(tokens.shape)
    weighted = grad_hidden * norm_gain
    average = jnp.mean(weighted * tokens_float, axis=3, keepdims=True)
    grad_tokens = (
        upstream_float + inverse_rms * weighted - tokens_float * inverse_rms**3 * average
    ).astype(jnp.bfloat16)
    return (output, grad_tokens, grad_one, grad_two, grad_three)


def solution(mesh):
    token_spec = P("sa", "sb", None, None)
    block_spec = P("sb", "sa", None, None)
    in_specs = (token_spec, P(), P(ALL, None), block_spec, token_spec, token_spec, token_spec)
    out_specs = (token_spec, token_spec, block_spec, token_spec, token_spec)
    return jax.shard_map(body, mesh=mesh, in_specs=in_specs, out_specs=out_specs, check_vma=False)
```

time: 581 us -> 909 us (1.56)
  waiting for transfers between devices: 53.3 us -> 560 us
  blocking collectives: 359 us -> 216 us
  local copies, waits for them, and re-layouts: 87.8 us -> 35.9 us
  starting transfers between devices: 27.6 us -> 44 us
    all_gather x6 -> x1, waiting for transfers between devices: 31.8 us -> 518 us  [body(): gathered = lax.all_gather(gate_weight, ALL, axis=0, tiled=True)]
    all_gather x19 -> x2, blocking collectives: 224 us -> 95.2 us  [the longest x1 54.3 us: body(): block_one = lax.all_gather(level_one[:, 0], 'sb', axis=0, tiled=True)]
    concatenate x1 -> x0, local copies, waits for them, and re-layouts: 37.8 us -> none  [gather_all_axes(): return laid_out(jnp.concatenate(outs, axis=widest + 1), dim)]
    all_to_all x4 -> x5, waiting for transfers between devices: 21.3 us -> 41.7 us  [the longest x1 23.5 us: from_blocks(): parts = lax.all_to_all(parts, ALL, split_axis=0, concat_axis=0, tiled=True)]
    all_to_all x4 -> x5, starting transfers between devices: 27.4 us -> 44 us  [the longest x1 12.6 us: body(): lax.all_to_all(block_two, 'sa', split_axis=1, concat_axis=0, tiled=True)]
    all_to_all x4 -> x2, blocking collectives: 134 us -> 121 us  [the longest x1 72.7 us: to_blocks(): parts = lax.all_to_all(parts, ALL, split_axis=0, concat_axis=0, tiled=True)]
    transpose x4 -> x3, local copies, waits for them, and re-layouts: 14.9 us -> 3.45 us  [the longest x2 3.4 us: to_blocks(): parts = parts.reshape(sa, sb, i, j, c // sb).transpose(0, 2, 1, 3, 4)]
    all_to_all x9 -> x3, local copies, waits for them, and re-layouts: 11.3 us -> 0.93 us  [the longest x1 0.51 us: body(): lax.all_to_all(packed, 'sb', split_axis=0, concat_axis=0, tiled=True)]
  transfers between devices with their start and end apart: 10 -> 6, of which waited for: 2 -> 5; matrix products, arithmetic and copies ran while one was open for 14% -> 3% of each run, Pallas kernels for 0% -> 0%
where the time goes in v1:
time: 909 us; the launch traced here: 907 us
  waiting for transfers between devices  560 us (62%)
  blocking collectives  216 us (24%)
  starting transfers between devices  44 us (5%)
  local copies, waits for them, and re-layouts  35.9 us (4%)
  matrix products  30.1 us (3%)
  between operations  14.4 us (2%)
    all_gather x1, waiting for transfers between devices, body(): gathered = lax.all_gather(gate_weight, ALL, axis=0, tiled=True)  518 us
    all_to_all x1, blocking collectives, to_blocks(): parts = lax.all_to_all(parts, ALL, split_axis=0, concat_axis=0, tiled=True)  72.7 us
    all_gather x1, blocking collectives, body(): block_one = lax.all_gather(level_one[:, 0], 'sb', axis=0, tiled=True)  54.3 us
    all_to_all x1, blocking collectives, from_blocks(): parts = lax.all_to_all(parts, ALL, split_axis=0, concat_axis=0, tiled=True)  48.4 us
    all_gather x1, blocking collectives, body(): block_two = lax.all_gather(level_two, 'sb', axis=1, tiled=True)  40.9 us
    dot_general x11, matrix products, dot(): return jnp.einsum(pattern, left, right, preferred_element_type=jnp.float32)  30.1 us
    all_to_all x1, waiting for transfers between devices, from_blocks(): parts = lax.all_to_all(parts, ALL, split_axis=0, concat_axis=0, tiled=True)  23.5 us
  transfers between devices with their start and end apart: 6, of which 5 were waited for; matrix products, arithmetic and copies ran while one was open for 3% of the time, Pallas kernels for 0%

profile of v1, /device:TPU:9, one launch (start us, length us, event | category | flops | bytes accessed | tf_op | source)
XLA Modules:
  0.0 906.5 jit_solution(1630995716396295364)
XLA Ops:
  8.8 40.9 %all_gather.10 = bf16[2,32,32,32]{3,2,0,1:T(8,128)(2,1)S(1)} all-gather(bf16[2,4,32,32]{3,2,0,1:T(8,128)(2,1)S(1)} %copy.129), channel_id=1, replica_groups=mesh['sa'=32,'sb'=8] {'sb'}, dimensions={1}, use_global_device_ids=true | all-gather | bytes 147456 | tf_op jit(solution)/shard_map/all_gather | solution.py:41
  50.8 12.6 %all-to-all-start.1 = ((bf16[32,2,1024]{2,1,0:T(2,128)(2,1)}), bf16[32,2,1024]{2,1,0:T(2,128)(2,1)S(1)}, u32[]{:S(2)}, u32[]{:S(2)}) async-start(bf16[32,2,1024]{2,1,0:T(2,128)(2,1)} %reshape.141), calls=%async_computation.1 | async-start | bytes 262144 | tf_op jit(solution)/shard_map/all_to_all | solution.py:42
  65.9 6.0 all-to-all-done.1
  71.9 10.5 %all-to-all-start = ((bf16[256,8,256]{2,1,0:T(8,128)(2,1)}), bf16[256,8,256]{2,1,0:T(8,128)(2,1)S(1)}, u32[]{:S(2)}, u32[]{:S(2)}) async-start(bf16[256,8,256]{2,1,0:T(8,128)(2,1)} %copy.154), calls=%async_computation | async-start | bytes 2097152 | tf_op jit(solution)/shard_map/all_to_all | solution.py:15
  82.4 54.3 %all-gather = bf16[32,1,64,64]{3,2,1,0:T(8,128)(2,1)S(1)} all-gather(bf16[4,1,64,64]{3,2,1,0:T(8,128)(2,1)S(1)} %copy-done.11), channel_id=2, replica_groups=mesh['sa'=32,'sb'=8] {'sb'}, dimensions={0}, use_global_device_ids=true | all-gather | bytes 294912 | tf_op jit(solution)/shard_map/all_gather | solution.py:40
  143.0 48.4 %all_to_all.59 = bf16[256,8,256]{2,1,0:T(8,128)(2,1)S(1)} all-to-all(bf16[256,8,256]{2,1,0:T(8,128)(2,1)S(1)} %copy.132), channel_id=1, replica_groups=mesh['sa'=32,'sb'=8] {'sa','sb'}, dimensions={0} | all-to-all | bytes 2097152 | tf_op jit(solution)/shard_map/all_to_all | solution.py:25
  194.1 1.8 convolution_bitcast_fusion
  195.9 517.8 %all-gather.3.cloned.1.call-done = bf16[2048,2048]{1,0:T(8,128)(2,1)} async-done(((bf16[8,2048]{1,0:T(8,128)(2,1)}), bf16[2048,2048]{1,0:T(8,128)(2,1)}) %all-gather.3.cloned.1.call-update) | async-done | bytes 8388624 | tf_op jit(solution)/shard_map/all_gather | solution.py:38
  713.8 9.3 %fusion.10 = (bf16[2,4,32,2048]{3,2,1,0:T(8,128)(2,1)S(1)}, bf16[2,4,32,2048]{3,2,1,0:T(8,128)(2,1)}, f32[2,4,32,2048]{3,2,1,0:T(8,128)}) fusion(bf16[2,4,32,2048]{3,2,1,0:T(8,128)(2,1)} %param.13, f32[2,4,32,2048]{3,2,1,0:T(8,128)} %convolution_bitcast_fusion, bf16[2,4,32,2048]{3,2,1,0:T(8,128)(2,1)} %param.7, ...), kind=kOutput, calls=%fused_computation.16 | convolution fusion | flops 2155347968 | bytes 16786432 | tf_op jit(solution)/shard_map/tr,rc->tc/dot_general | solution.py:31
  724.7 72.7 %all_to_all.60 = bf16[256,8,256]{2,1,0:T(8,128)(2,1)S(1)} all-to-all(bf16[256,8,256]{2,1,0:T(8,128)(2,1)S(1)} %copy.156), channel_id=1, replica_groups=mesh['sa'=32,'sb'=8] {'sa','sb'}, dimensions={0} | all-to-all | bytes 2097152 | tf_op jit(solution)/shard_map/all_to_all | solution.py:15
  797.6 2.3 copy.137
  799.9 2.1 reshape.131
  802.1 2.9 fusion.27
  805.5 2.2 reshape.143
  807.7 5.5 all-to-all-start.5
  816.3 5.6 all-to-all-done.5
  827.5 2.0 reshape.145
  829.5 5.1 all-to-all-start.6
  834.6 1.9 fusion.24
  840.2 6.5 all-to-all-done.6
  846.7 10.3 %all-to-all-start.4 = ((bf16[256,8,256]{2,1,0:T(8,128)(2,1)}), bf16[256,8,256]{2,1,0:T(8,128)(2,1)}, u32[]{:S(2)}, u32[]{:S(2)}) async-start(bf16[256,8,256]{2,1,0:T(8,128)(2,1)} %copy.142), calls=%async_computation.4 | async-start | bytes 2097152 | tf_op jit(solution)/shard_map/all_to_all | solution.py:25
  858.1 2.6 reshape.146
  863.2 23.5 %all-to-all-done.4 = bf16[256,8,256]{2,1,0:T(8,128)(2,1)} async-done(((bf16[256,8,256]{2,1,0:T(8,128)(2,1)}), bf16[256,8,256]{2,1,0:T(8,128)(2,1)}, u32[]{:S(2)}, u32[]{:S(2)}) %all-to-all-start.4) | async-done | bytes 1048608 | tf_op jit(solution)/shard_map/all_to_all | solution.py:25
  889.7 8.4 fusion.21
  (74 shorter events, 36.7 us)
Async XLA Ops:
  7.2 187.0 %copy-start = (bf16[2,4,32,32]{3,2,1,0:T(8,128)(2,1)S(1)}, bf16[2,4,32,32]{3,2,1,0:T(8,128)(2,1)}, u32[]{:S(2)}) copy-start(bf16[2,4,32,32]{3,2,1,0:T(8,128)(2,1)} %param.12) | copy-start | bytes 49156
  7.2 56.2 %copy-start.2 = (bf16[2,4,32,2048]{3,2,1,0:T(8,128)(2,1)S(1)}, bf16[2,4,32,2048]{3,2,1,0:T(8,128)(2,1)}, u32[]{:S(2)}) copy-start(bf16[2,4,32,2048]{3,2,1,0:T(8,128)(2,1)} %param.7) | copy-start | bytes 3145732
  7.2 56.5 %copy-start.12 = (f32[2048]{0:T(1024)S(1)}, f32[2048]{0:T(1024)}, u32[]{:S(2)}) copy-start(f32[2048]{0:T(1024)} %param.8) | copy-start | bytes 24580
  7.2 706.6 %all-gather.3.cloned.1.call-start = ((), (), s32[]{:S(2)}) async-start(), calls=%async_computation.7 | async-start | bytes 8421376 | tf_op jit(solution)/shard_map/all_gather | solution.py:38
  50.8 21.1 %all-to-all-start.1 = ((bf16[32,2,1024]{2,1,0:T(2,128)(2,1)}), bf16[32,2,1024]{2,1,0:T(2,128)(2,1)S(1)}, u32[]{:S(2)}, u32[]{:S(2)}) async-start(bf16[32,2,1024]{2,1,0:T(2,128)(2,1)} %reshape.141), calls=%async_computation.1 | async-start | bytes 262144 | tf_op jit(solution)/shard_map/all_to_all | solution.py:42
  64.4 18.1 %copy-start.11 = (bf16[4,1,64,64]{3,2,1,0:T(8,128)(2,1)S(1)}, bf16[4,1,64,64]{3,2,1,0:T(8,128)(2,1)}, u32[]{:S(2)}) copy-start(bf16[4,1,64,64]{3,2,1,0:T(8,128)(2,1)} %param.10) | copy-start | bytes 98308
  71.9 65.1 %all-to-all-start = ((bf16[256,8,256]{2,1,0:T(8,128)(2,1)}), bf16[256,8,256]{2,1,0:T(8,128)(2,1)S(1)}, u32[]{:S(2)}, u32[]{:S(2)}) async-start(bf16[256,8,256]{2,1,0:T(8,128)(2,1)} %copy.154), calls=%async_computation | async-start | bytes 2097152 | tf_op jit(solution)/shard_map/all_to_all | solution.py:15
  136.7 2.0 copy-start.6
  137.0 2.2 copy-start.4
  723.1 1.0 copy-start.8
  802.1 2.9 copy-start.1
  802.1 2.9 copy-start.5
  807.7 14.2 %all-to-all-start.5 = ((bf16[32,2,1024]{2,1,0:T(2,128)(2,1)}), bf16[32,2,1024]{2,1,0:T(2,128)(2,1)}, u32[]{:S(2)}, u32[]{:S(2)}) async-start(bf16[32,2,1024]{2,1,0:T(2,128)(2,1)} %reshape.143), calls=%async_computation.5 | async-start | bytes 262144 | tf_op jit(solution)/shard_map/all_to_all | solution.py:74
  823.2 11.4 %copy-start.7 = (bf16[32,1,64,64]{3,2,1,0:T(8,128)(2,1)S(1)}, bf16[32,1,64,64]{3,2,1,0:T(8,128)(2,1)}, u32[]{:S(2)}) copy-start(bf16[32,1,64,64]{3,2,1,0:T(8,128)(2,1)} %copy-done.6) | copy-start | bytes 786436
  829.5 17.2 %all-to-all-start.6 = ((bf16[8,2,12288]{2,1,0:T(2,128)(2,1)}), bf16[8,2,12288]{2,1,0:T(2,128)(2,1)}, u32[]{:S(2)}, u32[]{:S(2)}) async-start(bf16[8,2,12288]{2,1,0:T(2,128)(2,1)} %reshape.145), calls=%async_computation.6 | async-start | bytes 786432 | tf_op jit(solution)/shard_map/all_to_all | solution.py:85
  838.6 18.4 %copy-start.9 = (bf16[2,4,32,2048]{3,2,1,0:T(8,128)(2,1)S(1)}, bf16[2,4,32,2048]{3,2,1,0:T(8,128)(2,1)}, u32[]{:S(2)}) copy-start(bf16[2,4,32,2048]{3,2,1,0:T(8,128)(2,1)} %copy-done.8) | copy-start | bytes 3145732
  846.7 40.0 %all-to-all-start.4 = ((bf16[256,8,256]{2,1,0:T(8,128)(2,1)}), bf16[256,8,256]{2,1,0:T(8,128)(2,1)}, u32[]{:S(2)}, u32[]{:S(2)}) async-start(bf16[256,8,256]{2,1,0:T(8,128)(2,1)} %copy.142), calls=%async_computation.4 | async-start | bytes 2097152 | tf_op jit(solution)/shard_map/all_to_all | solution.py:25
  888.1 1.5 copy-start.3
  889.7 8.5 copy-start.10
Sparse Core Ops, SparseCore 0:
  9.9 703.8 all-gather.2
